TPU v7x, 32 devices: a whole 2x2x4 slice. The times are simulated.
32 devices in a mesh: gx: 4 (over y, x), gy: 2 (over core), gz: 4 (over z).
Axes of the slice: x: 2, y: 2, z: 4, core: 2. Of those that a mesh axis runs over, the one named last changes fastest.
Arguments:
- pair: bfloat16 [128, 1024, 1024], P('gz', 'gy', 'gx'), may hold values from -6 to 6
- pair_mask: int32 [1024, 1024], P('gy', 'gx'), may hold values 0 or 1
- in_gain: float32 [128], replicated, may hold values from 0.5 to 2
- w_left: bfloat16 [128, 128], P(None, 'gz'), may hold values from -0.5 to 0.5
- w_left_gate: bfloat16 [128, 128], P(None, 'gz'), may hold values from -0.5 to 0.5
- w_right: bfloat16 [128, 128], P(None, 'gz'), may hold values from -0.5 to 0.5
- w_right_gate: bfloat16 [128, 128], P(None, 'gz'), may hold values from -0.5 to 0.5
- w_out_gate: bfloat16 [128, 128], P(None, 'gz'), may hold values from -0.5 to 0.5
- out_gain: float32 [128], P('gz'), may hold values from 0.5 to 2
- w_out: bfloat16 [128, 128], P(None, 'gz'), may hold values from -0.5 to 0.5
Outputs:
- update: bfloat16 [128, 1024, 1024], P('gz', 'gy', 'gx')
All inputs are finite; a program needn't handle non-finite values. No bound on the sum of `pair_mask` on one device may be relied on, other than what follows from the above.
Results may differ from a plain program's by a relative error of at most 0.0078.
Values may be sent and summed in bfloat16 or wider, within the bound.
A program may use at most 192 MiB of HBM per device.

v0:
```python
import functools
import itertools
import math

import jax
import jax.numpy as jnp
from jax import lax
from jax.experimental import pallas as pl
from jax.experimental.pallas import tpu as pltpu
from jax.sharding import PartitionSpec as P

epsilon = 1e-05
MESH = pl.DeviceIdType.MESH


def exchange_kernel(axes, sizes, take, put, x_ref, o_ref, send_sem, recv_sem, local_sem):
    me = tuple(lax.axis_index(axis) for axis in axes)
    offsets = [o for o in itertools.product(*(range(n) for n in sizes)) if any(o)]

    def peer_of(offset):
        return tuple(lax.rem(m + o, n) for m, o, n in zip(me, offset, sizes))

    barrier = pltpu.get_barrier_semaphore()
    for offset in offsets:
        pl.semaphore_signal(
            barrier, inc=1, device_id=dict(zip(axes, peer_of(offset))), device_id_type=MESH
        )
    pl.semaphore_wait(barrier, len(offsets))
    copies = []
    for index, offset in enumerate(offsets):
        peer = peer_of(offset)
        copy = pltpu.make_async_remote_copy(
            src_ref=take(x_ref, peer),
            dst_ref=put(o_ref, me),
            send_sem=send_sem.at[index],
            recv_sem=recv_sem.at[index],
            device_id=dict(zip(axes, peer)),
            device_id_type=MESH,
        )
        copy.start()
        copies.append(copy)
    own = pltpu.make_async_copy(take(x_ref, me), put(o_ref, me), local_sem)
    own.start()
    own.wait()
    for copy in copies:
        copy.wait()


def exchange(x, axes, shape, take, put, collective_id):
    sizes = tuple(lax.axis_size(axis) for axis in axes)
    count = math.prod(sizes) - 1
    moved = x.size * x.dtype.itemsize
    return pl.pallas_call(
        functools.partial(exchange_kernel, axes, sizes, take, put),
        out_shape=jax.ShapeDtypeStruct(shape, x.dtype),
        in_specs=[pl.BlockSpec(memory_space=pl.ANY)],
        out_specs=pl.BlockSpec(memory_space=pl.ANY),
        scratch_shapes=[
            pltpu.SemaphoreType.DMA((count,)),
            pltpu.SemaphoreType.DMA((count,)),
            pltpu.SemaphoreType.DMA,
        ],
        compiler_params=pltpu.CompilerParams(collective_id=collective_id, has_side_effects=True),
        cost_estimate=pl.CostEstimate(flops=0, bytes_accessed=20 * moved, transcendentals=0),
    )(x)


def normalize(values, gain):
    average = jnp.mean(values, axis=0, keepdims=True)
    centered = values - average
    spread = jnp.mean(jnp.square(centered), axis=0, keepdims=True)
    return (centered * lax.rsqrt(spread + epsilon) * gain).astype(jnp.bfloat16)


def project_kernel(x_ref, mask_ref, gain_ref, weight_ref, left_ref, right_ref, gate_ref):
    rows = x_ref.shape[0]
    h = left_ref.shape[1]
    gain = gain_ref[...]

    def body(row, carry):
        normed = normalize(x_ref[row].astype(jnp.float32), gain)
        mask = mask_ref[pl.ds(row, 1), :]

        def part(index):
            return jnp.dot(
                weight_ref[index * h : (index + 1) * h, :],
                normed,
                preferred_element_type=jnp.float32,
            )

        left_ref[row] = (mask * jax.nn.sigmoid(part(1)) * part(0)).astype(jnp.bfloat16)
        right_ref[row] = (mask * jax.nn.sigmoid(part(3)) * part(2)).astype(jnp.bfloat16)
        gate_ref[row] = jax.nn.sigmoid(part(4)).astype(jnp.bfloat16)
        return carry

    lax.fori_loop(0, rows, body, 0)


def finish_kernel(mix_ref, gate_ref, gain_ref, weight_ref, out_ref):
    gain = gain_ref[...]

    def body(row, carry):
        normed = normalize(mix_ref[row].astype(jnp.float32), gain)
        projected = jnp.dot(weight_ref[...], normed, preferred_element_type=jnp.float32)
        out_ref[row] = (gate_ref[row].astype(jnp.float32) * projected).astype(jnp.bfloat16)
        return carry

    lax.fori_loop(0, mix_ref.shape[0], body, 0)


def local(
    pair,
    pair_mask,
    in_gain,
    w_left,
    w_left_gate,
    w_right,
    w_right_gate,
    w_out_gate,
    out_gain,
    w_out,
):
    nx, nz = lax.axis_size("gx"), lax.axis_size("gz")
    channels, i_rows, k_columns = pair.shape
    c_all = channels * nz
    rows = i_rows // nz
    h_all = w_left.shape[1] * nz
    h_own = h_all // (nx * nz)
    stacked = jnp.stack([w_left, w_left_gate, w_right, w_right_gate, w_out_gate, w_out])
    weights = jnp.swapaxes(lax.all_gather(stacked, "gz", axis=2, tiled=True), 1, 2)
    gain_mix = lax.all_gather(out_gain, "gz", axis=0, tiled=True)
    mask_rows = lax.dynamic_slice_in_dim(
        pair_mask, lax.axis_index("gz") * rows, rows, axis=0
    ).astype(jnp.float32)

    gathered = exchange(
        jnp.swapaxes(pair, 0, 1),
        ("gz",),
        (rows, c_all, k_columns),
        lambda ref, dev: ref.at[pl.ds(dev[0] * rows, rows)],
        lambda ref, dev: ref.at[:, pl.ds(pl.multiple_of(dev[0] * channels, channels), channels)],
        0,
    )

    block = 8
    row_spec = pl.BlockSpec((block, c_all, k_columns), lambda i: (i, 0, 0))
    h_spec = pl.BlockSpec((block, h_all, k_columns), lambda i: (i, 0, 0))
    whole = lambda *shape: pl.BlockSpec(shape, lambda i: (0,) * len(shape))
    h_shape = jax.ShapeDtypeStruct((rows, h_all, k_columns), jnp.bfloat16)
    left_rows, right_rows, out_gate = pl.pallas_call(
        project_kernel,
        grid=(rows // block,),
        out_shape=(h_shape, h_shape, h_shape),
        in_specs=[
            row_spec,
            pl.BlockSpec((block, k_columns), lambda i: (i, 0)),
            whole(c_all, 1),
            whole(5 * h_all, c_all),
        ],
        out_specs=(h_spec, h_spec, h_spec),
    )(gathered, mask_rows, in_gain[:, None], weights[:5].reshape(5 * h_all, c_all))

    def block_of(ref, dev):
        return ref.at[
            :,
            pl.ds(pl.multiple_of(dev[1] * rows, rows), rows),
            pl.ds(pl.multiple_of(dev[0] * k_columns, k_columns), k_columns),
        ]

    def heads_of(ref, dev):
        return ref.at[pl.ds((dev[0] * nz + dev[1]) * h_own, h_own)]

    group_shape = (h_own, i_rows, k_columns * nx)
    right_group = exchange(
        jnp.swapaxes(right_rows, 0, 1), ("gx", "gz"), group_shape, heads_of, block_of, 1
    )
    right_all = lax.all_gather(right_group, "gy", axis=1, tiled=True)
    left_group = exchange(
        jnp.swapaxes(left_rows, 0, 1), ("gx", "gz"), group_shape, heads_of, block_of, 2
    )
    mixed = lax.dot_general(
        left_group,
        right_all,
        (((2,), (2,)), ((0,), (0,))),
        preferred_element_type=jnp.float32,
    ).astype(jnp.bfloat16)
    mix = exchange(
        mixed, ("gx", "gz"), (h_all, rows, k_columns), block_of, heads_of, 3
    )
    update = pl.pallas_call(
        finish_kernel,
        grid=(rows // block,),
        out_shape=h_shape,
        in_specs=[h_spec, h_spec, whole(h_all, 1), whole(h_all, h_all)],
        out_specs=h_spec,
    )(jnp.swapaxes(mix, 0, 1), out_gate, gain_mix[:, None], weights[5])
    result = exchange(
        update,
        ("gz",),
        (i_rows, channels, k_columns),
        lambda ref, dev: ref.at[:, pl.ds(pl.multiple_of(dev[0] * channels, channels), channels)],
        lambda ref, dev: ref.at[pl.ds(dev[0] * rows, rows)],
        4,
    )
    return jnp.swapaxes(result, 0, 1)


def solution(mesh):
    placed = (
        P("gz", "gy", "gx"),
        P("gy", "gx"),
        P(),
        P(None, "gz"),
        P(None, "gz"),
        P(None, "gz"),
        P(None, "gz"),
        P(None, "gz"),
        P("gz"),
        P(None, "gz"),
    )
    return jax.shard_map(
        local, mesh=mesh, in_specs=placed, out_specs=P("gz", "gy", "gx"), check_vma=False
    )
```

profile of v0, /device:TPU:11, one launch (start us, length us, event | category | flops | bytes accessed | tf_op | source)
XLA Modules:
  0.0 1111.4 jit_solution(16889234583801824666)
XLA Ops:
  6.5 0.0 all-gather.2.cloned.1.call-start
  6.5 0.7 constant_dynamic-update-slice_fusion.5
  7.2 1.4 copy.12.gain_ref
  8.6 0.7 constant_dynamic-update-slice_fusion.4
  9.3 0.7 constant_dynamic-update-slice_fusion.3
  10.0 0.7 constant_dynamic-update-slice_fusion.2
  10.7 0.7 constant_dynamic-update-slice_fusion.1
  11.4 0.7 constant_dynamic-update-slice_fusion
  12.1 10.9 all_gather.9
  23.0 0.7 slice.8
  23.7 11.5 %copy.25 = bf16[32,512,256]{2,0,1:T(8,128)(2,1)} copy(bf16[32,512,256]{2,1,0:T(8,128)(2,1)} %param.10) | data formatting | bytes 16777216 | tf_op args[0]
  35.2 182.9 %shard_map.100.x_ref = bf16[128,128,256]{2,1,0:T(8,128)(2,1)} custom-call(bf16[512,32,256]{2,1,0:T(8,128)(2,1)} %bitcast.38), custom_call_target="tpu_custom_call" | custom-call | bytes 167772160 | tf_op jit(solution)/shard_map/pallas_call | solution.py:53
  218.2 1.6 dynamic-slice_convert_fusion.mask_ref
  219.7 43.1 %shard_map.101 = (bf16[128,128,256]{2,1,0:T(8,128)(2,1)}, bf16[128,128,256]{2,1,0:T(8,128)(2,1)}, bf16[128,128,256]{2,1,0:T(8,128)(2,1)}) custom-call(bf16[128,128,256]{2,1,0:T(8,128)(2,1)} %shard_map.100.x_ref, f32[128,256]{1,0:T(8,128)} %dynamic-slice_convert_fusion.mask_ref, f32[128,1]{1,0:T(8,128)} %copy.12.gain_ref, bf16[640,128]{1,0:T(8,128)(2,1)} %bitcast.41), custom_call_target="tpu_custom_call" | custom-call | tf_op jit(solution)/shard_map/pallas_call | solution.py:150
  262.8 11.4 %copy.23 = bf16[128,128,256]{2,0,1:T(8,128)(2,1)} copy(bf16[128,128,256]{2,1,0:T(8,128)(2,1)} %get-tuple-element.9) | data formatting | bytes 16777216 | tf_op jit(solution)/shard_map/pallas_call | solution.py:150
  274.2 184.0 %shard_map.103 = bf16[8,512,1024]{2,1,0:T(8,128)(2,1)} custom-call(bf16[128,128,256]{2,1,0:T(8,128)(2,1)} %bitcast.35), custom_call_target="tpu_custom_call" | custom-call | bytes 167772160 | tf_op jit(solution)/shard_map/pallas_call | solution.py:53
  458.2 0.0 copy-start.1
  458.2 0.0 copy-start
  458.2 0.0 all-gather.2.cloned.1.call-update
  458.2 0.6 copy-done.1
  458.8 0.6 dynamic-slice
  460.0 0.0 copy-done
  460.0 0.2 dynamic-update-slice
  460.2 4.9 all-reduce
  465.2 0.7 copy.16.gain_ref
  465.9 15.6 %copy.24 = bf16[128,128,256]{2,0,1:T(8,128)(2,1)} copy(bf16[128,128,256]{2,1,0:T(8,128)(2,1)} %get-tuple-element.8) | data formatting | bytes 16777216 | tf_op jit(solution)/shard_map/pallas_call | solution.py:150
  481.5 186.2 %shard_map.102 = bf16[8,512,1024]{2,1,0:T(8,128)(2,1)} custom-call(bf16[128,128,256]{2,1,0:T(8,128)(2,1)} %bitcast.36), custom_call_target="tpu_custom_call" | custom-call | bytes 167772160 | tf_op jit(solution)/shard_map/pallas_call | solution.py:53
  667.7 0.6 slice_bitcast_fusion.weight_ref
  668.3 0.0 all-gather.2.cloned.1.call-done
  668.3 15.8 %convolution_convert_fusion.x_ref = bf16[8,512,1024]{2,1,0:T(8,128)(2,1)} fusion(bf16[8,512,1024]{2,1,0:T(8,128)(2,1)} %shard_map.102, bf16[8,1024,1024]{2,1,0:T(8,128)(2,1)} %all-gather.2.cloned.1.call-done), kind=kOutput, calls=%fused_computation.4 | convolution fusion | flops 8594128896 | bytes 33554432 | tf_op jit(solution)/shard_map/dot_general | solution.py:181
  684.1 184.0 %shard_map.104 = bf16[128,128,256]{2,1,0:T(8,128)(2,1)} custom-call(bf16[8,512,1024]{2,1,0:T(8,128)(2,1)} %convolution_convert_fusion.x_ref), custom_call_target="tpu_custom_call" | custom-call | bytes 167772160 | tf_op jit(solution)/shard_map/pallas_call | solution.py:53
  868.0 11.5 %copy.22 = bf16[128,128,256]{2,0,1:T(8,128)(2,1)} copy(bf16[128,128,256]{2,1,0:T(8,128)(2,1)} %shard_map.104) | data formatting | bytes 16777216 | tf_op jit(solution)/shard_map/pallas_call | solution.py:53
  879.6 31.5 %shard_map.105.x_ref = bf16[128,128,256]{2,1,0:T(8,128)(2,1)} custom-call(bf16[128,128,256]{2,1,0:T(8,128)(2,1)} %bitcast.34, bf16[128,128,256]{2,1,0:T(8,128)(2,1)} %get-tuple-element.10.gate_ref, f32[128,1]{1,0:T(8,128)} %copy.16.gain_ref, bf16[128,128]{1,0:T(8,128)(2,1)} %slice_bitcast_fusion.weight_ref), custom_call_target="tpu_custom_call" | custom-call | tf_op jit(solution)/shard_map/pallas_call | solution.py:190
  911.1 181.9 %shard_map.106 = bf16[512,32,256]{2,1,0:T(8,128)(2,1)} custom-call(bf16[128,128,256]{2,1,0:T(8,128)(2,1)} %shard_map.105.x_ref), custom_call_target="tpu_custom_call" | custom-call | bytes 167772160 | tf_op jit(solution)/shard_map/pallas_call | solution.py:53
  1093.0 11.5 %copy.17 = bf16[32,512,256]{2,1,0:T(8,128)(2,1)} copy(bf16[32,512,256]{2,0,1:T(8,128)(2,1)} %bitcast.37) | data formatting | bytes 16777216 | tf_op jit(solution)/shard_map/transpose | solution.py:205
  (1 shorter events, 0.0 us)
Async XLA Ops:
  6.5 661.8 %all-gather.2.cloned.1.call-start = ((), (), s32[]{:S(2)}) async-start(), calls=%async_computation | async-start | bytes 25165824 | tf_op jit(solution)/shard_map/all_gather | solution.py:177
  458.2 0.7 copy-start.1
  458.2 1.8 copy-start
Sparse Core Ops, SparseCore 0:
  458.4 31.6 all-gather.1
where the time goes:
time: 1110 us
  Pallas kernels  994 us (90%)
  local copies, waits for them, and re-layouts  70.6 us (6%)
  blocking collectives  15.8 us (1%)
  matrix products  15.8 us (1%)
  between operations  14 us (1%)
    pallas_call x5, Pallas kernels, exchange(): pl.pallas_call(functools.partial(exchange_kernel, axes, sizes, take, put)...  919 us
    pallas_call x1, Pallas kernels, local(): pl.pallas_call(project_kernel, grid=(rows // block,), out_shape=(h_shape,...  43.1 us
    pallas_call x1, Pallas kernels, local(): pl.pallas_call(finish_kernel, grid=(rows // block,), out_shape=h_shape, i...  31.5 us
    pallas_call x2, local copies, waits for them, and re-layouts, local(): pl.pallas_call(project_kernel, grid=(rows // block,), out_shape=(h_shape,...  26.9 us
  transfers between devices with their start and end apart: 1, of which 0 were waited for; matrix products, arithmetic and copies ran while one was open for 2% of the time, Pallas kernels for 17%

commit v1 on v0

v1 whole, which is shorter than its diff:
```python
import functools

import jax
import jax.numpy as jnp
from jax import lax
from jax.experimental import pallas as pl
from jax.experimental.pallas import tpu as pltpu
from jax.sharding import PartitionSpec as P

epsilon = 1e-05
MESH = pl.DeviceIdType.MESH
LANES = 128
GROUP = 16
PITCH = GROUP + 1
VMEM_LIMIT = 67043328


def normalize(values, gain):
    average = jnp.mean(values, axis=0, keepdims=True)
    centered = values - average
    spread = jnp.mean(jnp.square(centered), axis=0, keepdims=True)
    return (centered * lax.rsqrt(spread + epsilon) * gain).astype(jnp.bfloat16)


class Place:
    def __init__(self, nx, ny, nz):
        self.nx, self.ny, self.nz = nx, ny, nz
        self.gx, self.gy, self.gz = (lax.axis_index(a) for a in ("gx", "gy", "gz"))
        self.group = self.gx * ny + self.gy
        self.groups = nx * ny
        self.side = self.gz // (nz // 2)
        self.mid = nz // 2 - 1 + self.side
        self.far = self.side * (nz - 1)
        self.is_mid = self.gz == self.mid
        self.is_far = jnp.logical_and(self.gz == self.far, jnp.logical_not(self.is_mid))

    def member(self, offset):
        q = lax.rem(self.group + offset, self.groups)
        return q, q // self.ny, lax.rem(q, self.ny)


def remote(src, dst, send, recv, **device):
    return pltpu.make_async_remote_copy(
        src_ref=src, dst_ref=dst, send_sem=send, recv_sem=recv, device_id=device, device_id_type=MESH
    )


def turn_out(slab, stage_of, count):
    def body(i, carry):
        for u in range(8):
            h = i * 8 + u
            for part in range(slab.shape[0]):
                rows = slab.at[part][pl.ds(h * PITCH, GROUP), :]
                stage_of(h, part, rows.astype(jnp.bfloat16))
        return carry

    lax.fori_loop(0, count // 8, body, 0)


def put_strided(slab, row, values):
    for part in range(slab.shape[0]):
        slab.at[part][pl.ds(row, values.shape[0], stride=PITCH), :] = values[
            :, part * LANES : (part + 1) * LANES
        ]


def project_kernel(
    dims,
    pair_ref,
    mask_ref,
    gain_ref,
    weight_ref,
    right_ref,
    left_ref,
    gate_ref,
    raw,
    right_stage,
    left_stage,
    gate_stage,
    right_slab,
    left_slab,
    raw_send,
    raw_recv,
    own_sem,
    right_send,
    left_send,
    right_recv,
    left_recv,
    gate_sem,
):
    nx, ny, nz, near, away = dims
    at = Place(nx, ny, nz)
    rows, c, k = pair_ref.shape
    h = weight_ref.shape[0] // 5
    size = right_stage.shape[2]
    chunks = rows // size
    half = chunks // 2
    per = near + away
    ahead = min(4, chunks)

    def row_of(t, side):
        return pl.multiple_of(lax.rem(t + side * half, chunks) * size, size)

    def raw_copy(t, side):
        r = row_of(t, side)
        return remote(
            pair_ref.at[pl.ds(r, size)],
            raw.at[pl.ds(r, size), pl.ds(pl.multiple_of(at.gz * c, c), c)],
            raw_send.at[t, side],
            raw_recv.at[lax.rem(t + side * half, chunks), at.gz],
            gz=nz // 2 - 1 + side,
        )

    def raw_wait(t, z):
        r = row_of(t, at.side)
        remote(
            pair_ref.at[pl.ds(r, size)],
            raw.at[pl.ds(r, size), pl.ds(pl.multiple_of(z * c, c), c)],
            raw_send.at[t, 0],
            raw_recv.at[lax.rem(t + at.side * half, chunks), z],
            gz=z,
        ).wait_recv()

    def sends(stage, out_ref, block, send, recv, slot, r):
        first = pl.multiple_of(at.gy * block + r, size)
        where = (pl.ds(first, size), pl.ds(pl.multiple_of(at.gx * k, k), k))
        found = []
        for o in range(at.groups):
            q, qx, qy = at.member(o)
            src = stage.at[slot, pl.ds(q * per, near)]
            dst = out_ref.at[(pl.ds(0, near),) + where]
            if o == 0:
                found.append((pltpu.make_async_copy(src, dst, send.at[slot, 0]), True))
            else:
                found.append((remote(src, dst, send.at[slot, o], recv.at[at.group], gx=qx, gy=qy), False))
            if away:
                found.append(
                    (
                        remote(
                            stage.at[slot, pl.ds(q * per + near, away)],
                            out_ref.at[(pl.ds(0, away),) + where],
                            send.at[slot, at.groups + o],
                            recv.at[at.group],
                            gx=qx,
                            gy=qy,
                            gz=at.far,
                        ),
                        False,
                    )
                )
        return found

    def right_sends(t):
        return sends(
            right_stage, right_ref, rows, right_send, right_recv, lax.rem(t, 2), row_of(t, at.side)
        )

    def left_sends(t):
        return sends(left_stage, left_ref, rows // 2, left_send, left_recv, lax.rem(t, 2), t * size)

    def gate_copy(t):
        slot = lax.rem(t, 2)
        return pltpu.make_async_copy(
            gate_stage.at[slot], gate_ref.at[pl.ds(t * size, size)], gate_sem.at[slot]
        )

    def start(copies):
        for copy, _ in copies:
            copy.start()

    def drain(copies):
        for copy, is_local in copies:
            if is_local:
                copy.wait()
            else:
                copy.wait_send()

    def compute(t, with_left):
        slot = lax.rem(t, 2)
        r0 = row_of(t, at.side)
        gain = gain_ref[...]
        for g in range(size // GROUP):

            def body(r, carry):
                row = r0 + g * GROUP + r
                normed = normalize(raw[row].astype(jnp.float32), gain)
                mask = mask_ref[pl.ds(row, 1), :]

                def part(index):
                    return jnp.dot(
                        weight_ref[index * h : (index + 1) * h, :],
                        normed,
                        preferred_element_type=jnp.float32,
                    )

                put_strided(right_slab, r, mask * jax.nn.sigmoid(part(3)) * part(2))
                if with_left:
                    put_strided(left_slab, r, mask * jax.nn.sigmoid(part(1)) * part(0))
                    gate_stage[slot, g * GROUP + r] = jax.nn.sigmoid(part(4)).astype(jnp.bfloat16)
                return carry

            lax.fori_loop(0, GROUP, body, 0)

            def stage_into(stage):
                def put(head, part, values):
                    stage[
                        slot,
                        head,
                        g * GROUP : (g + 1) * GROUP,
                        part * LANES : (part + 1) * LANES,
                    ] = values

                return put

            turn_out(right_slab, stage_into(right_stage), h)
            if with_left:
                turn_out(left_slab, stage_into(left_stage), h)

    def arrive(t):
        for o in range(1, nz):
            raw_wait(t, lax.rem(at.gz + o, nz))

    @pl.when(jnp.logical_not(at.is_mid))
    def _():
        def begin(t, carry):
            raw_copy(t, 0).start()
            raw_copy(t, 1).start()
            return carry

        def end(t, carry):
            raw_copy(t, 0).wait_send()
            raw_copy(t, 1).wait_send()
            return carry

        lax.fori_loop(0, chunks, begin, 0)
        lax.fori_loop(0, chunks, end, 0)

    @pl.when(at.is_mid)
    def _():
        other = 1 - at.side
        own = pltpu.make_async_copy(
            pair_ref, raw.at[:, pl.ds(pl.multiple_of(at.gz * c, c), c)], own_sem
        )
        own.start()
        for t in range(ahead):
            raw_copy(t, other).start()
        own.wait()

        def step(t, with_left):
            @pl.when(t + ahead < chunks)
            def _():
                raw_copy(t + ahead, other).start()

            arrive(t)

            @pl.when(t >= 2)
            def _():
                drain(right_sends(t - 2))
                if with_left:
                    drain(left_sends(t - 2))
                    gate_copy(t - 2).wait()

            compute(t, with_left)
            start(right_sends(t))
            if with_left:
                start(left_sends(t))
                gate_copy(t).start()

        def first(t, carry):
            step(t, True)
            return carry

        def second(t, carry):
            step(t, False)
            return carry

        lax.fori_loop(0, half, first, 0)
        lax.fori_loop(half, chunks, second, 0)
        for t in range(max(half - 2, 0), half):
            drain(left_sends(t))
            gate_copy(t).wait()
        for t in range(max(chunks - 2, 0), chunks):
            drain(right_sends(t))

        def end(t, carry):
            raw_copy(t, other).wait_send()
            return carry

        lax.fori_loop(0, chunks, end, 0)

    def collect(heads, first_offset):
        for o in range(first_offset, at.groups):
            q, qx, qy = at.member(o)
            for out_ref, block, recv in (
                (right_ref, rows, right_recv),
                (left_ref, rows // 2, left_recv),
            ):
                whole = out_ref.at[
                    pl.ds(0, heads),
                    pl.ds(pl.multiple_of(qy * block, block), block),
                    pl.ds(pl.multiple_of(qx * k, k), k),
                ]
                remote(whole, whole, own_sem, recv.at[q], gz=at.mid).wait_recv()

    @pl.when(at.is_mid)
    def _():
        collect(near, 1)

    if away:

        @pl.when(at.is_far)
        def _():
            collect(away, 0)


def mix_kernel(
    dims,
    right_ref,
    left_ref,
    gate_ref,
    gain_ref,
    weight_ref,
    out_ref,
    right,
    left,
    stage,
    mix,
    gate,
    out_stage,
    in_slab,
    out_slab,
    right_sem,
    left_sem,
    gate_sem,
    mix_send,
    mix_recv,
    out_send,
    out_recv,
):
    nx, ny, nz, near, away = dims
    at = Place(nx, ny, nz)
    c, rows, k = out_ref.shape
    h = weight_ref.shape[0]
    own_rows = rows // 2
    steps = own_rows // GROUP
    per = near + away
    deep = max(near, away)

    def left_copies(t, heads):
        slot = lax.rem(t, 2)
        return [
            pltpu.make_async_copy(
                left_ref.at[pl.ds(0, heads), pl.ds(pl.multiple_of(y * own_rows + t * GROUP, GROUP), GROUP)],
                left.at[slot, pl.ds(0, heads), pl.ds(y * GROUP, GROUP)],
                left_sem.at[slot, y],
            )
            for y in range(ny)
        ]

    def right_copy(head):
        return pltpu.make_async_copy(right_ref.at[head], right.at[head], right_sem.at[head])

    def gate_copy(t):
        slot = lax.rem(t, 2)
        return pltpu.make_async_copy(
            gate_ref.at[pl.ds(t * GROUP, GROUP)], gate.at[slot], gate_sem.at[slot]
        )

    def mix_sends(t, heads, shift, first_offset):
        slot = lax.rem(t, 2)
        found = []
        for o in range(first_offset, at.groups):
            q, qx, qy = at.member(o)
            found.append(
                remote(
                    stage.at[
                        slot,
                        pl.ds(0, heads),
                        pl.ds(pl.multiple_of(qy * GROUP, GROUP), GROUP),
                        pl.ds(pl.multiple_of(qx * k, k), k),
                    ],
                    mix.at[
                        pl.ds(at.group * per + shift, heads),
                        pl.ds(pl.multiple_of(t * GROUP, GROUP), GROUP),
                    ],
                    mix_send.at[slot, o],
                    mix_recv.at[t],
                    gx=qx,
                    gy=qy,
                    gz=at.mid,
                )
            )
        return found

    def multiply(t, heads, shift, first_offset):
        slot = lax.rem(t, 2)

        @pl.when(t + 1 < steps)
        def _():
            for copy in left_copies(t + 1, heads):
                copy.start()

        for copy in left_copies(t, heads):
            copy.wait()

        @pl.when(t >= 2)
        def _():
            for copy in mix_sends(t - 2, heads, shift, first_offset):
                copy.wait_send()

        def body(head, carry):
            @pl.when(t == 0)
            def _():
                right_copy(head).wait()

            product = lax.dot_general(
                left[slot, head],
                right[head],
                (((1,), (1,)), ((), ())),
                preferred_element_type=jnp.float32,
            )
            stage[slot, head] = product.astype(jnp.bfloat16)
            return carry

        lax.fori_loop(0, heads, body, 0)
        for copy in mix_sends(t, heads, shift, first_offset):
            copy.start()

    def begin(heads):
        for copy in left_copies(0, heads):
            copy.start()
        for head in range(heads):
            right_copy(head).start()

    def end(heads, shift, first_offset):
        for t in range(max(steps - 2, 0), steps):
            for copy in mix_sends(t, heads, shift, first_offset):
                copy.wait_send()

    def out_copies(t):
        slot = lax.rem(t, 2)
        where = pl.ds(pl.multiple_of(at.side * own_rows + t * GROUP, GROUP), GROUP)
        found = [
            (
                pltpu.make_async_copy(
                    out_stage.at[slot, pl.ds(pl.multiple_of(at.gz * c, c), c)],
                    out_ref.at[:, where],
                    out_send.at[slot, 0],
                ),
                True,
            )
        ]
        for o in range(1, nz):
            z = lax.rem(at.gz + o, nz)
            found.append(
                (
                    remote(
                        out_stage.at[slot, pl.ds(pl.multiple_of(z * c, c), c)],
                        out_ref.at[:, where],
                        out_send.at[slot, o],
                        out_recv.at[at.side],
                        gz=z,
                    ),
                    False,
                )
            )
        return found

    def drain_out(t):
        for copy, is_local in out_copies(t):
            if is_local:
                copy.wait()
            else:
                copy.wait_send()

    def finish(t):
        slot = lax.rem(t, 2)
        here = pl.ds(pl.multiple_of(t * GROUP, GROUP), GROUP)
        if h > near:
            rest = mix.at[pl.ds(0, h - near), here]
            remote(rest, rest, out_send.at[0, 0], mix_recv.at[t], gz=at.mid).wait_recv()

        gain = gain_ref[...]

        def turn_in(i, carry):
            for u in range(8):
                head = i * 8 + u
                for part in range(in_slab.shape[0]):
                    in_slab.at[part][pl.ds(head * PITCH, GROUP), :] = mix[
                        head, here, part * LANES : (part + 1) * LANES
                    ].astype(jnp.float32)
            return carry

        lax.fori_loop(0, h // 8, turn_in, 0)

        @pl.when(t + 1 < steps)
        def _():
            gate_copy(t + 1).start()

        gate_copy(t).wait()

        def body(r, carry):
            values = jnp.concatenate(
                [
                    in_slab.at[part][pl.ds(r, h, stride=PITCH), :]
                    for part in range(in_slab.shape[0])
                ],
                axis=1,
            )
            normed = normalize(values, gain)
            projected = jnp.dot(weight_ref[...], normed, preferred_element_type=jnp.float32)
            put_strided(out_slab, r, gate[slot, r].astype(jnp.float32) * projected)
            return carry

        lax.fori_loop(0, GROUP, body, 0)

        @pl.when(t >= 2)
        def _():
            drain_out(t - 2)

        def put(head, part, values):
            out_stage[slot, head, :, part * LANES : (part + 1) * LANES] = values

        turn_out(out_slab, put, h)
        for copy, _ in out_copies(t):
            copy.start()

    @pl.when(at.is_mid)
    def _():
        begin(near)
        gate_copy(0).start()

        def keep_own(t):
            slot = lax.rem(t, 2)
            mix[
                pl.ds(at.group * per, near), pl.ds(pl.multiple_of(t * GROUP, GROUP), GROUP)
            ] = stage[
                slot,
                0:near,
                pl.ds(pl.multiple_of(at.gy * GROUP, GROUP), GROUP),
                pl.ds(pl.multiple_of(at.gx * k, k), k),
            ]

        def step(t, carry):
            multiply(t, near, 0, 1)
            keep_own(t)

            @pl.when(t >= 1)
            def _():
                finish(t - 1)

            return carry

        lax.fori_loop(0, steps, step, 0)
        finish(jnp.int32(steps - 1))
        end(near, 0, 1)
        for t in range(max(steps - 2, 0), steps):
            drain_out(t)

    if away:

        @pl.when(at.is_far)
        def _():
            begin(away)

            def step(t, carry):
                multiply(t, away, near, 0)
                return carry

            lax.fori_loop(0, steps, step, 0)
            end(away, near, 0)

    for side in range(2):
        source = nz // 2 - 1 + side

        @pl.when(at.gz != source)
        def _():
            where = out_ref.at[:, pl.ds(side * own_rows, own_rows)]
            remote(where, where, out_send.at[0, 0], out_recv.at[side], gz=source).wait_recv()


def local(
    pair,
    pair_mask,
    in_gain,
    w_left,
    w_left_gate,
    w_right,
    w_right_gate,
    w_out_gate,
    out_gain,
    w_out,
):
    nx, ny, nz = (lax.axis_size(a) for a in ("gx", "gy", "gz"))
    c, rows, k = pair.shape
    c_all = c * nz
    h = w_left.shape[1] * nz
    groups = nx * ny
    per = h // groups
    away = 0 if nz < 4 else max(1, per * 5 // 16)
    near = per - away
    deep = max(near, away)
    dims = (nx, ny, nz, near, away)
    size = min(32, rows // 2)
    chunks = rows // size
    steps = rows // 2 // GROUP
    parts = k // LANES

    stacked = jnp.stack([w_left, w_left_gate, w_right, w_right_gate, w_out_gate, w_out])
    weights = jnp.swapaxes(lax.all_gather(stacked, "gz", axis=2, tiled=True), 1, 2)
    gain_mix = lax.all_gather(out_gain, "gz", axis=0, tiled=True)
    anywhere = pl.BlockSpec(memory_space=pl.ANY)
    vmem = pl.BlockSpec(memory_space=pltpu.VMEM)
    bf16 = lambda *shape: jax.ShapeDtypeStruct(shape, jnp.bfloat16)
    sem = pltpu.SemaphoreType.DMA
    slab = pltpu.VMEM((parts, h * PITCH, LANES), jnp.float32)
    params = pltpu.CompilerParams(has_side_effects=True, vmem_limit_bytes=VMEM_LIMIT)

    right, left, gate = pl.pallas_call(
        functools.partial(project_kernel, dims),
        out_shape=(
            bf16(deep, ny * rows, nx * k),
            bf16(deep, ny * rows // 2, nx * k),
            bf16(rows // 2, h, k),
        ),
        in_specs=[anywhere, vmem, vmem, vmem],
        out_specs=(anywhere, anywhere, anywhere),
        scratch_shapes=[
            pltpu.VMEM((rows, c_all, k), jnp.bfloat16),
            pltpu.VMEM((2, h, size, k), jnp.bfloat16),
            pltpu.VMEM((2, h, size, k), jnp.bfloat16),
            pltpu.VMEM((2, size, h, k), jnp.bfloat16),
            slab,
            slab,
            sem((chunks, 2)),
            sem((chunks, nz)),
            sem,
            sem((2, 2 * groups)),
            sem((2, 2 * groups)),
            sem((groups,)),
            sem((groups,)),
            sem((2,)),
        ],
        compiler_params=params,
    )(
        jnp.swapaxes(pair, 0, 1),
        pair_mask.astype(jnp.float32),
        in_gain[:, None],
        weights[:5].reshape(5 * h, c_all),
    )

    return pl.pallas_call(
        functools.partial(mix_kernel, dims),
        out_shape=bf16(c, rows, k),
        in_specs=[anywhere, anywhere, anywhere, vmem, vmem],
        out_specs=anywhere,
        scratch_shapes=[
            pltpu.VMEM((deep, ny * rows, nx * k), jnp.bfloat16),
            pltpu.VMEM((2, deep, ny * GROUP, nx * k), jnp.bfloat16),
            pltpu.VMEM((2, deep, ny * GROUP, ny * rows), jnp.bfloat16),
            pltpu.VMEM((h, rows // 2, k), jnp.bfloat16),
            pltpu.VMEM((2, GROUP, h, k), jnp.bfloat16),
            pltpu.VMEM((2, h, GROUP, k), jnp.bfloat16),
            slab,
            slab,
            sem((deep,)),
            sem((2, ny)),
            sem((2,)),
            sem((2, groups)),
            sem((steps,)),
            sem((2, nz)),
            sem((2,)),
        ],
        compiler_params=params,
    )(right, left, gate, gain_mix[:, None], weights[5])


def solution(mesh):
    placed = (
        P("gz", "gy", "gx"),
        P("gy", "gx"),
        P(),
        P(None, "gz"),
        P(None, "gz"),
        P(None, "gz"),
        P(None, "gz"),
        P(None, "gz"),
        P("gz"),
        P(None, "gz"),
    )
    return jax.shard_map(
        local, mesh=mesh, in_specs=placed, out_specs=P("gz", "gy", "gx"), check_vma=False
    )
```

time: 1110 us -> 736 us (0.66)
  Pallas kernels: 994 us -> 686 us
  local copies, waits for them, and re-layouts: 70.6 us -> 28.9 us
  matrix products: 15.8 us -> 0 us
  between operations: 14 us -> 0.68 us
    pallas_call x7 -> x2, Pallas kernels: 994 us -> 686 us  [the longest x1 423 us: local(): pl.pallas_call(functools.partial(project_kernel, dims), out_shape=(bf16(d...]
    pallas_call x3 -> x0, local copies, waits for them, and re-layouts: 38.5 us -> none  [the longest x2 26.9 us: local(): pl.pallas_call(project_kernel, grid=(rows // block,), out_shape=(h_shape,...]
    dot_general x1 -> x0, matrix products: 15.8 us -> none  [local(): lax.dot_general(left_group, right_all, (((2,), (2,)), ((0,), (0,))), pref...]
    transpose x1 -> x0, local copies, waits for them, and re-layouts: 11.5 us -> none  [local(): return jnp.swapaxes(result, 0, 1)]
    unnamed x13 -> x10, local copies, waits for them, and re-layouts: 16.5 us -> 24.8 us
  transfers between devices with their start and end apart: 1 -> 0, of which waited for: 0 -> 0; matrix products, arithmetic and copies ran while one was open for 2% -> 0% of each run, Pallas kernels for 17% -> 0%
where the time goes in v1:
time: 736 us; the launch traced here: 735 us
  Pallas kernels  686 us (93%)
  local copies, waits for them, and re-layouts  28.9 us (4%)
  blocking collectives  17.7 us (2%)
    pallas_call x1, Pallas kernels, local(): pl.pallas_call(functools.partial(project_kernel, dims), out_shape=(bf16(d...  423 us
    pallas_call x1, Pallas kernels, local(): pl.pallas_call(functools.partial(mix_kernel, dims), out_shape=bf16(c, row...  263 us
    unnamed x10, local copies, waits for them, and re-layouts  24.8 us

profile of v1, /device:TPU:11, one launch (start us, length us, event | category | flops | bytes accessed | tf_op | source)
XLA Modules:
  0.0 735.5 jit_solution(8300925413268552634)
XLA Ops:
  0.0 1.2 dynamic-slice
  1.9 0.9 dynamic-update-slice
  2.8 7.2 all-reduce
  10.0 0.7 constant_dynamic-update-slice_fusion.5
  10.7 0.7 constant_dynamic-update-slice_fusion.4
  11.4 0.7 constant_dynamic-update-slice_fusion.3
  12.1 0.7 constant_dynamic-update-slice_fusion.2
  12.8 0.7 constant_dynamic-update-slice_fusion.1
  13.5 0.7 constant_dynamic-update-slice_fusion
  14.2 0.7 copy.13.gain_ref
  14.9 1.4 copy.12.gain_ref
  16.3 10.5 %all_gather.6 = bf16[6,128,128]{1,2,0:T(8,128)(2,1)S(1)} all-gather(bf16[6,128,32]{1,2,0:T(8,128)(2,1)S(1)} %constant_dynamic-update-slice_fusion), channel_id=1, replica_groups=mesh['gx'=4,'gy'=2,'gz'=4] {'gz'}, dimensions={2}, use_global_device_ids=true | all-gather | bytes 245760 | tf_op jit(solution)/shard_map/all_gather | solution.py:610
  26.8 0.6 slice_bitcast_fusion.weight_ref
  27.4 0.7 slice.8
  28.1 1.9 convert_element_type.3.mask_ref
  29.9 11.5 %copy.15 = bf16[32,512,256]{2,0,1:T(8,128)(2,1)} copy(bf16[32,512,256]{2,1,0:T(8,128)(2,1)} %param.10) | data formatting | bytes 16777216 | tf_op args[0]
  41.5 423.4 %shard_map.100 = (bf16[11,1024,1024]{2,1,0:T(8,128)(2,1)}, bf16[11,512,1024]{2,1,0:T(8,128)(2,1)}, bf16[256,128,256]{2,1,0:T(8,128)(2,1)}) custom-call(bf16[512,32,256]{2,1,0:T(8,128)(2,1)} %bitcast.22, f32[512,256]{1,0:T(8,128)} %convert_element_type.3.mask_ref, f32[128,1]{1,0:T(8,128)} %copy.12.gain_ref, bf16[640,128]{1,0:T(8,128)(2,1)} %bitcast.25), custom_call_target="tpu_custom_call" | custom-call | tf_op jit(solution)/shard_map/pallas_call | solution.py:619
  464.9 262.9 %shard_map.101 = bf16[32,512,256]{2,1,0:T(8,128)(2,1)} custom-call(bf16[11,1024,1024]{2,1,0:T(8,128)(2,1)} %get-tuple-element.8.right_ref, bf16[11,512,1024]{2,1,0:T(8,128)(2,1)} %get-tuple-element.9.left_ref, bf16[256,128,256]{2,1,0:T(8,128)(2,1)} %get-tuple-element.10.gate_ref, f32[128,1]{1,0:T(8,128)} %copy.13.gain_ref, ...), custom_call_target="tpu_custom_call" | custom-call | tf_op jit(solution)/shard_map/pallas_call | solution.py:652
  727.8 7.7 %copy.23 = bf16[32,512,256]{2,1,0:T(8,128)(2,1)} copy(bf16[32,512,256]{2,1,0:T(8,128)(2,1)} %shard_map.101) | data formatting | bytes 16777216
  (1 shorter events, 0.0 us)

commit v2 on v1

--- a/solution.py
+++ b/solution.py
@@ -12,6 +12,8 @@
 LANES = 128
 GROUP = 16
 PITCH = GROUP + 1
+SLOTS = 4
+LAG = 3
 VMEM_LIMIT = 67043328
 
 
@@ -45,6 +47,33 @@
     )
 
 
+def same_place(n):
+    return lax.broadcasted_iota(jnp.int32, (n, n), 0) == lax.broadcasted_iota(jnp.int32, (n, n), 1)
+
+
+def column(row):
+    return jnp.sum(jnp.where(same_place(row.shape[1]), row, 0.0), axis=1, keepdims=True)
+
+
+def turn_in(slab, source, count):
+    def body(i, carry):
+        for u in range(8):
+            channel = i * 8 + u
+            for part in range(slab.shape[0]):
+                slab.at[part][pl.ds(channel * PITCH, GROUP), :] = source(channel, part).astype(
+                    jnp.float32
+                )
+        return carry
+
+    lax.fori_loop(0, count // 8, body, 0)
+
+
+def get_strided(slab, row, count):
+    return jnp.concatenate(
+        [slab.at[part][pl.ds(row, count, stride=PITCH), :] for part in range(slab.shape[0])], axis=1
+    )
+
+
 def turn_out(slab, stage_of, count):
     def body(i, carry):
         for u in range(8):
@@ -69,18 +98,26 @@
     pair_ref,
     mask_ref,
     gain_ref,
-    weight_ref,
+    w0_ref,
+    w1_ref,
+    w2_ref,
+    w3_ref,
+    w4_ref,
     right_ref,
     left_ref,
     gate_ref,
     raw,
+    weight_ref,
     right_stage,
     left_stage,
     gate_stage,
+    raw_slab,
     right_slab,
     left_slab,
     raw_send,
     raw_recv,
+    weight_send,
+    weight_recv,
     own_sem,
     right_send,
     left_send,
@@ -90,13 +127,15 @@
 ):
     nx, ny, nz, near, away = dims
     at = Place(nx, ny, nz)
-    rows, c, k = pair_ref.shape
-    h = weight_ref.shape[0] // 5
+    c, rows, k = pair_ref.shape
+    given = (w0_ref, w1_ref, w2_ref, w3_ref, w4_ref)
+    h_z, c_all = w0_ref.shape
+    h = h_z * nz
     size = right_stage.shape[2]
     chunks = rows // size
     half = chunks // 2
     per = near + away
-    ahead = min(4, chunks)
+    ahead = min(6, chunks)
 
     def row_of(t, side):
         return pl.multiple_of(lax.rem(t + side * half, chunks) * size, size)
@@ -104,8 +143,8 @@
     def raw_copy(t, side):
         r = row_of(t, side)
         return remote(
-            pair_ref.at[pl.ds(r, size)],
-            raw.at[pl.ds(r, size), pl.ds(pl.multiple_of(at.gz * c, c), c)],
+            pair_ref.at[:, pl.ds(r, size)],
+            raw.at[pl.ds(pl.multiple_of(at.gz * c, c), c), pl.ds(r, size)],
             raw_send.at[t, side],
             raw_recv.at[lax.rem(t + side * half, chunks), at.gz],
             gz=nz // 2 - 1 + side,
@@ -114,12 +153,24 @@
     def raw_wait(t, z):
         r = row_of(t, at.side)
         remote(
-            pair_ref.at[pl.ds(r, size)],
-            raw.at[pl.ds(r, size), pl.ds(pl.multiple_of(z * c, c), c)],
+            pair_ref.at[:, pl.ds(r, size)],
+            raw.at[pl.ds(pl.multiple_of(z * c, c), c), pl.ds(r, size)],
             raw_send.at[t, 0],
             raw_recv.at[lax.rem(t + at.side * half, chunks), z],
             gz=z,
         ).wait_recv()
+
+    def weight_rows(index, z):
+        return weight_ref.at[index, pl.ds(pl.multiple_of(z * h_z, h_z), h_z)]
+
+    def weight_copy(index, side):
+        return remote(
+            given[index],
+            weight_rows(index, at.gz),
+            weight_send.at[side, index],
+            weight_recv.at[at.gz, index],
+            gz=nz // 2 - 1 + side,
+        )
 
     def sends(stage, out_ref, block, send, recv, slot, r):
         first = pl.multiple_of(at.gy * block + r, size)
@@ -152,11 +203,11 @@
 
     def right_sends(t):
         return sends(
-            right_stage, right_ref, rows, right_send, right_recv, lax.rem(t, 2), row_of(t, at.side)
+            right_stage, right_ref, rows, right_send, right_recv, lax.rem(t, SLOTS), row_of(t, at.side)
         )
 
     def left_sends(t):
-        return sends(left_stage, left_ref, rows // 2, left_send, left_recv, lax.rem(t, 2), t * size)
+        return sends(left_stage, left_ref, rows // 2, left_send, left_recv, lax.rem(t, SLOTS), t * size)
 
     def gate_copy(t):
         slot = lax.rem(t, 2)
@@ -176,19 +227,26 @@
                 copy.wait_send()
 
     def compute(t, with_left):
-        slot = lax.rem(t, 2)
+        slot = lax.rem(t, SLOTS)
+        gate_slot = lax.rem(t, 2)
         r0 = row_of(t, at.side)
-        gain = gain_ref[...]
+        gain = column(gain_ref[...])
         for g in range(size // GROUP):
+            here = pl.ds(pl.multiple_of(r0 + g * GROUP, GROUP), GROUP)
+            turn_in(
+                raw_slab,
+                lambda channel, part: raw[channel, here, part * LANES : (part + 1) * LANES],
+                c_all,
+            )
 
             def body(r, carry):
                 row = r0 + g * GROUP + r
-                normed = normalize(raw[row].astype(jnp.float32), gain)
-                mask = mask_ref[pl.ds(row, 1), :]
+                normed = normalize(get_strided(raw_slab, r, c_all), gain)
+                mask = mask_ref[pl.ds(row, 1), :].astype(jnp.float32)
 
                 def part(index):
                     return jnp.dot(
-                        weight_ref[index * h : (index + 1) * h, :],
+                        weight_ref[index],
                         normed,
                         preferred_element_type=jnp.float32,
                     )
@@ -196,7 +254,7 @@
                 put_strided(right_slab, r, mask * jax.nn.sigmoid(part(3)) * part(2))
                 if with_left:
                     put_strided(left_slab, r, mask * jax.nn.sigmoid(part(1)) * part(0))
-                    gate_stage[slot, g * GROUP + r] = jax.nn.sigmoid(part(4)).astype(jnp.bfloat16)
+                    gate_stage[gate_slot, g * GROUP + r] = jax.nn.sigmoid(part(4)).astype(jnp.bfloat16)
                 return carry
 
             lax.fori_loop(0, GROUP, body, 0)
@@ -227,6 +285,10 @@
             raw_copy(t, 1).start()
             return carry
 
+        for index in range(5):
+            weight_copy(index, 0).start()
+            weight_copy(index, 1).start()
+
         def end(t, carry):
             raw_copy(t, 0).wait_send()
             raw_copy(t, 1).wait_send()
@@ -234,17 +296,40 @@
 
         lax.fori_loop(0, chunks, begin, 0)
         lax.fori_loop(0, chunks, end, 0)
+        for index in range(5):
+            weight_copy(index, 0).wait_send()
+            weight_copy(index, 1).wait_send()
 
     @pl.when(at.is_mid)
     def _():
         other = 1 - at.side
         own = pltpu.make_async_copy(
-            pair_ref, raw.at[:, pl.ds(pl.multiple_of(at.gz * c, c), c)], own_sem
+            pair_ref, raw.at[pl.ds(pl.multiple_of(at.gz * c, c), c)], own_sem
         )
+        own_weights = [
+            pltpu.make_async_copy(
+                given[index], weight_rows(index, at.gz), weight_recv.at[at.gz, index]
+            )
+            for index in range(5)
+        ]
+        for index in range(5):
+            weight_copy(index, other).start()
+            own_weights[index].start()
         own.start()
         for t in range(ahead):
             raw_copy(t, other).start()
         own.wait()
+        for index in range(5):
+            own_weights[index].wait()
+            for o in range(1, nz):
+                z = lax.rem(at.gz + o, nz)
+                remote(
+                    given[index],
+                    weight_rows(index, z),
+                    weight_send.at[0, index],
+                    weight_recv.at[z, index],
+                    gz=z,
+                ).wait_recv()
 
         def step(t, with_left):
             @pl.when(t + ahead < chunks)
@@ -253,11 +338,16 @@
 
             arrive(t)
 
-            @pl.when(t >= 2)
+            @pl.when(t >= SLOTS)
             def _():
-                drain(right_sends(t - 2))
+                drain(right_sends(t - SLOTS))
                 if with_left:
-                    drain(left_sends(t - 2))
+                    drain(left_sends(t - SLOTS))
+
+            if with_left:
+
+                @pl.when(t >= 2)
+                def _():
                     gate_copy(t - 2).wait()
 
             compute(t, with_left)
@@ -277,9 +367,10 @@
         lax.fori_loop(0, half, first, 0)
         lax.fori_loop(half, chunks, second, 0)
         for t in range(max(half - 2, 0), half):
+            gate_copy(t).wait()
+        for t in range(max(half - SLOTS, 0), half):
             drain(left_sends(t))
-            gate_copy(t).wait()
-        for t in range(max(chunks - 2, 0), chunks):
+        for t in range(max(chunks - SLOTS, 0), chunks):
             drain(right_sends(t))
 
         def end(t, carry):
@@ -287,6 +378,8 @@
             return carry
 
         lax.fori_loop(0, chunks, end, 0)
+        for index in range(5):
+            weight_copy(index, other).wait_send()
 
     def collect(heads, first_offset):
         for o in range(first_offset, at.groups):
@@ -318,8 +411,8 @@
     right_ref,
     left_ref,
     gate_ref,
-    gain_ref,
-    weight_ref,
+    gain_part_ref,
+    w_out_ref,
     out_ref,
     right,
     left,
@@ -327,8 +420,13 @@
     mix,
     gate,
     out_stage,
+    gains_ref,
+    gain_ref,
+    weight_ref,
     in_slab,
     out_slab,
+    weight_send,
+    weight_recv,
     right_sem,
     left_sem,
     gate_sem,
@@ -340,7 +438,8 @@
     nx, ny, nz, near, away = dims
     at = Place(nx, ny, nz)
     c, rows, k = out_ref.shape
-    h = weight_ref.shape[0]
+    c_z, h = w_out_ref.shape
+    h_z = gain_part_ref.shape[1]
     own_rows = rows // 2
     steps = own_rows // GROUP
     per = near + away
@@ -367,7 +466,7 @@
         )
 
     def mix_sends(t, heads, shift, first_offset):
-        slot = lax.rem(t, 2)
+        slot = lax.rem(t, SLOTS)
         found = []
         for o in range(first_offset, at.groups):
             q, qx, qy = at.member(o)
@@ -393,7 +492,8 @@
         return found
 
     def multiply(t, heads, shift, first_offset):
-        slot = lax.rem(t, 2)
+        slot = lax.rem(t, SLOTS)
+        left_slot = lax.rem(t, 2)
 
         @pl.when(t + 1 < steps)
         def _():
@@ -403,9 +503,9 @@
         for copy in left_copies(t, heads):
             copy.wait()
 
-        @pl.when(t >= 2)
+        @pl.when(t >= SLOTS)
         def _():
-            for copy in mix_sends(t - 2, heads, shift, first_offset):
+            for copy in mix_sends(t - SLOTS, heads, shift, first_offset):
                 copy.wait_send()
 
         def body(head, carry):
@@ -414,7 +514,7 @@
                 right_copy(head).wait()
 
             product = lax.dot_general(
-                left[slot, head],
+                left[left_slot, head],
                 right[head],
                 (((1,), (1,)), ((), ())),
                 preferred_element_type=jnp.float32,
@@ -433,12 +533,12 @@
             right_copy(head).start()
 
     def end(heads, shift, first_offset):
-        for t in range(max(steps - 2, 0), steps):
+        for t in range(max(steps - SLOTS, 0), steps):
             for copy in mix_sends(t, heads, shift, first_offset):
                 copy.wait_send()
 
     def out_copies(t):
-        slot = lax.rem(t, 2)
+        slot = lax.rem(t, SLOTS)
         where = pl.ds(pl.multiple_of(at.side * own_rows + t * GROUP, GROUP), GROUP)
         found = [
             (
@@ -474,24 +574,19 @@
                 copy.wait_send()
 
     def finish(t):
-        slot = lax.rem(t, 2)
+        slot = lax.rem(t, SLOTS)
+        gate_slot = lax.rem(t, 2)
         here = pl.ds(pl.multiple_of(t * GROUP, GROUP), GROUP)
         if h > near:
             rest = mix.at[pl.ds(0, h - near), here]
             remote(rest, rest, out_send.at[0, 0], mix_recv.at[t], gz=at.mid).wait_recv()
 
         gain = gain_ref[...]
-
-        def turn_in(i, carry):
-            for u in range(8):
-                head = i * 8 + u
-                for part in range(in_slab.shape[0]):
-                    in_slab.at[part][pl.ds(head * PITCH, GROUP), :] = mix[
-                        head, here, part * LANES : (part + 1) * LANES
-                    ].astype(jnp.float32)
-            return carry
-
-        lax.fori_loop(0, h // 8, turn_in, 0)
+        turn_in(
+            in_slab,
+            lambda head, part: mix[head, here, part * LANES : (part + 1) * LANES],
+            h,
+        )
 
         @pl.when(t + 1 < steps)
         def _():
@@ -500,38 +595,82 @@
         gate_copy(t).wait()
 
         def body(r, carry):
-            values = jnp.concatenate(
-                [
-                    in_slab.at[part][pl.ds(r, h, stride=PITCH), :]
-                    for part in range(in_slab.shape[0])
-                ],
-                axis=1,
-            )
-            normed = normalize(values, gain)
+            normed = normalize(get_strided(in_slab, r, h), gain)
             projected = jnp.dot(weight_ref[...], normed, preferred_element_type=jnp.float32)
-            put_strided(out_slab, r, gate[slot, r].astype(jnp.float32) * projected)
+            put_strided(out_slab, r, gate[gate_slot, r].astype(jnp.float32) * projected)
             return carry
 
         lax.fori_loop(0, GROUP, body, 0)
 
-        @pl.when(t >= 2)
+        @pl.when(t >= SLOTS)
         def _():
-            drain_out(t - 2)
+            drain_out(t - SLOTS)
 
         def put(head, part, values):
             out_stage[slot, head, :, part * LANES : (part + 1) * LANES] = values
 
-        turn_out(out_slab, put, h)
+        turn_out(out_slab, put, c * nz)
         for copy, _ in out_copies(t):
             copy.start()
 
+    lag = min(LAG, steps)
+
+    def small(z):
+        return (
+            (gain_part_ref, gains_ref.at[z]),
+            (w_out_ref, weight_ref.at[pl.ds(pl.multiple_of(z * c_z, c_z), c_z)]),
+        )
+
+    def weight_copies(side):
+        return [
+            remote(
+                src,
+                dst,
+                weight_send.at[side, index],
+                weight_recv.at[at.gz, index],
+                gz=nz // 2 - 1 + side,
+            )
+            for index, (src, dst) in enumerate(small(at.gz))
+        ]
+
+    def own_weights():
+        return [
+            pltpu.make_async_copy(src, dst, weight_recv.at[at.gz, index])
+            for index, (src, dst) in enumerate(small(at.gz))
+        ]
+
+    def take_weights():
+        for copy in own_weights():
+            copy.wait()
+        for o in range(1, nz):
+            z = lax.rem(at.gz + o, nz)
+            for index, (src, dst) in enumerate(small(z)):
+                remote(
+                    src, dst, weight_send.at[0, index], weight_recv.at[z, index], gz=z
+                ).wait_recv()
+        for z in range(nz):
+            gain_ref[z * h_z : (z + 1) * h_z, :] = column(gains_ref[z])
+
+    @pl.when(jnp.logical_not(at.is_mid))
+    def _():
+        for side in range(2):
+            for copy in weight_copies(side):
+                copy.start()
+        for side in range(2):
+            for copy in weight_copies(side):
+                copy.wait_send()
+
     @pl.when(at.is_mid)
     def _():
+        for copy in weight_copies(1 - at.side):
+            copy.start()
+        for copy in own_weights():
+            copy.start()
         begin(near)
         gate_copy(0).start()
 
         def keep_own(t):
-            slot = lax.rem(t, 2)
+            slot = lax.rem(t, SLOTS)
             mix[
                 pl.ds(at.group * per, near), pl.ds(pl.multiple_of(t * GROUP, GROUP), GROUP)
             ] = stage[
@@ -545,17 +684,29 @@
             multiply(t, near, 0, 1)
             keep_own(t)
 
-            @pl.when(t >= 1)
+            @pl.when(t == lag)
             def _():
-                finish(t - 1)
+                take_weights()
+
+            @pl.when(t >= lag)
+            def _():
+                finish(t - lag)
 
             return carry
 
+        def last(t, carry):
+            finish(t)
+            return carry
+
         lax.fori_loop(0, steps, step, 0)
-        finish(jnp.int32(steps - 1))
+        if lag >= steps:
+            take_weights()
+        lax.fori_loop(steps - lag, steps, last, 0)
         end(near, 0, 1)
-        for t in range(max(steps - 2, 0), steps):
+        for t in range(max(steps - SLOTS, 0), steps):
             drain_out(t)
+        for copy in weight_copies(1 - at.side):
+            copy.wait_send()
 
     if away:
 
@@ -601,14 +752,11 @@
     near = per - away
     deep = max(near, away)
     dims = (nx, ny, nz, near, away)
-    size = min(32, rows // 2)
+    size = min(GROUP, rows // 2)
     chunks = rows // size
     steps = rows // 2 // GROUP
     parts = k // LANES
 
-    stacked = jnp.stack([w_left, w_left_gate, w_right, w_right_gate, w_out_gate, w_out])
-    weights = jnp.swapaxes(lax.all_gather(stacked, "gz", axis=2, tiled=True), 1, 2)
-    gain_mix = lax.all_gather(out_gain, "gz", axis=0, tiled=True)
     anywhere = pl.BlockSpec(memory_space=pl.ANY)
     vmem = pl.BlockSpec(memory_space=pltpu.VMEM)
     bf16 = lambda *shape: jax.ShapeDtypeStruct(shape, jnp.bfloat16)
@@ -623,56 +771,69 @@
             bf16(deep, ny * rows // 2, nx * k),
             bf16(rows // 2, h, k),
         ),
-        in_specs=[anywhere, vmem, vmem, vmem],
+        in_specs=[anywhere, vmem, vmem] + [anywhere] * 5,
         out_specs=(anywhere, anywhere, anywhere),
         scratch_shapes=[
-            pltpu.VMEM((rows, c_all, k), jnp.bfloat16),
-            pltpu.VMEM((2, h, size, k), jnp.bfloat16),
-            pltpu.VMEM((2, h, size, k), jnp.bfloat16),
+            pltpu.VMEM((c_all, rows, k), jnp.bfloat16),
+            pltpu.VMEM((5, h, c_all), jnp.bfloat16),
+            pltpu.VMEM((SLOTS, h, size, k), jnp.bfloat16),
+            pltpu.VMEM((SLOTS, h, size, k), jnp.bfloat16),
             pltpu.VMEM((2, size, h, k), jnp.bfloat16),
+            pltpu.VMEM((parts, c_all * PITCH, LANES), jnp.float32),
             slab,
             slab,
             sem((chunks, 2)),
             sem((chunks, nz)),
+            sem((2, 5)),
+            sem((nz, 5)),
             sem,
-            sem((2, 2 * groups)),
-            sem((2, 2 * groups)),
+            sem((SLOTS, 2 * groups)),
+            sem((SLOTS, 2 * groups)),
             sem((groups,)),
             sem((groups,)),
             sem((2,)),
         ],
         compiler_params=params,
     )(
-        jnp.swapaxes(pair, 0, 1),
-        pair_mask.astype(jnp.float32),
-        in_gain[:, None],
-        weights[:5].reshape(5 * h, c_all),
+        pair,
+        pair_mask,
+        in_gain[None, :],
+        w_left.T,
+        w_left_gate.T,
+        w_right.T,
+        w_right_gate.T,
+        w_out_gate.T,
     )
 
     return pl.pallas_call(
         functools.partial(mix_kernel, dims),
         out_shape=bf16(c, rows, k),
-        in_specs=[anywhere, anywhere, anywhere, vmem, vmem],
+        in_specs=[anywhere] * 5,
         out_specs=anywhere,
         scratch_shapes=[
             pltpu.VMEM((deep, ny * rows, nx * k), jnp.bfloat16),
             pltpu.VMEM((2, deep, ny * GROUP, nx * k), jnp.bfloat16),
-            pltpu.VMEM((2, deep, ny * GROUP, ny * rows), jnp.bfloat16),
+            pltpu.VMEM((SLOTS, deep, ny * GROUP, ny * rows), jnp.bfloat16),
             pltpu.VMEM((h, rows // 2, k), jnp.bfloat16),
             pltpu.VMEM((2, GROUP, h, k), jnp.bfloat16),
-            pltpu.VMEM((2, h, GROUP, k), jnp.bfloat16),
+            pltpu.VMEM((SLOTS, c_all, GROUP, k), jnp.bfloat16),
+            pltpu.VMEM((nz, 1, h // nz), jnp.float32),
+            pltpu.VMEM((h, 1), jnp.float32),
+            pltpu.VMEM((c_all, h), jnp.bfloat16),
             slab,
-            slab,
+            pltpu.VMEM((parts, c_all * PITCH, LANES), jnp.float32),
+            sem((2, 2)),
+            sem((nz, 2)),
             sem((deep,)),
             sem((2, ny)),
             sem((2,)),
-            sem((2, groups)),
+            sem((SLOTS, groups)),
             sem((steps,)),
-            sem((2, nz)),
+            sem((SLOTS, nz)),
             sem((2,)),
         ],
         compiler_params=params,
-    )(right, left, gate, gain_mix[:, None], weights[5])
+    )(right, left, gate, out_gain[None, :], w_out.T)
 
 
 def solution(mesh):

time: 736 us -> 667 us (0.906)
  Pallas kernels: 686 us -> 659 us
  local copies, waits for them, and re-layouts: 28.9 us -> 7.65 us
  blocking collectives: 17.7 us -> 0 us
    pallas_call x1, Pallas kernels: 423 us -> 404 us  [local(): pl.pallas_call(functools.partial(project_kernel, dims), out_shape=(bf16(d...]
    unnamed x10 -> x1, local copies, waits for them, and re-layouts: 24.8 us -> 7.65 us
    all_gather x1 -> x0, blocking collectives: 10.5 us -> none  [local(): lax.all_gather(stacked, 'gz', axis=2, tiled=True)]
    pallas_call x1, Pallas kernels: 263 us -> 255 us  [local(): pl.pallas_call(functools.partial(mix_kernel, dims), out_shape=bf16(c, row...]
where the time goes in v2:
time: 667 us
  Pallas kernels  659 us (99%)
  local copies, waits for them, and re-layouts  7.65 us (1%)
    pallas_call x1, Pallas kernels, local(): pl.pallas_call(functools.partial(project_kernel, dims), out_shape=(bf16(d...  404 us
    pallas_call x1, Pallas kernels, local(): pl.pallas_call(functools.partial(mix_kernel, dims), out_shape=bf16(c, row...  255 us

profile of v2, /device:TPU:11, one launch (start us, length us, event | category | flops | bytes accessed | tf_op | source)
XLA Modules:
  0.0 667.1 jit_solution(681503383489396132)
XLA Ops:
  0.0 404.4 %shard_map.100 = (bf16[11,1024,1024]{2,1,0:T(8,128)(2,1)}, bf16[11,512,1024]{2,1,0:T(8,128)(2,1)}, bf16[256,128,256]{2,1,0:T(8,128)(2,1)}) custom-call(bf16[32,512,256]{2,1,0:T(8,128)(2,1)} %pair_ref.1, s32[512,256]{1,0:T(8,128)} %mask_ref.1, f32[1,128]{1,0:T(1,128)} %bitcast.15, bf16[32,128]{1,0:T(8,128)(2,1)} %bitcast.9, bf16[32,128]{1,0:T(8,128)(2,1)} %bitcast.10, ...), custom_call_target="tpu_custom_call" | custom-call | tf_op jit(solution)/shard_map/pallas_call | solution.py:767
  404.4 255.0 %shard_map.101 = bf16[32,512,256]{2,1,0:T(8,128)(2,1)} custom-call(bf16[11,1024,1024]{2,1,0:T(8,128)(2,1)} %get-tuple-element.8.right_ref, bf16[11,512,1024]{2,1,0:T(8,128)(2,1)} %get-tuple-element.9.left_ref, bf16[256,128,256]{2,1,0:T(8,128)(2,1)} %get-tuple-element.10.gate_ref, f32[1,32]{1,0:T(1,128)} %bitcast.14, bf16[32,128]{1,0:T(8,128)(2,1)} %bitcast.8), custom_call_target="tpu_custom_call" | custom-call | tf_op jit(solution)/shard_map/pallas_call | solution.py:808
  659.5 7.7 %copy.12 = bf16[32,512,256]{2,1,0:T(8,128)(2,1)} copy(bf16[32,512,256]{2,1,0:T(8,128)(2,1)} %shard_map.101) | data formatting | bytes 16777216

commit v3 on v0

v3 whole, which is shorter than its diff:
```python
import functools

import jax
import jax.numpy as jnp
from jax import lax
from jax.experimental import pallas as pl
from jax.experimental.pallas import tpu as pltpu
from jax.sharding import PartitionSpec as P

epsilon = 1e-05
MESH = pl.DeviceIdType.MESH
LANES = 128
GROUP = 16
PITCH = GROUP + 1
SLOTS = 4
LAG = 2
WIDE = 2
VMEM_LIMIT = 67043328


def normalize(values, gain):
    average = jnp.mean(values, axis=0, keepdims=True)
    centered = values - average
    spread = jnp.mean(jnp.square(centered), axis=0, keepdims=True)
    return (centered * lax.rsqrt(spread + epsilon) * gain).astype(jnp.bfloat16)


class Place:
    def __init__(self, nx, ny, nz):
        self.nx, self.ny, self.nz = nx, ny, nz
        self.gx, self.gy, self.gz = (lax.axis_index(a) for a in ("gx", "gy", "gz"))
        self.group = self.gx * ny + self.gy
        self.groups = nx * ny
        self.side = self.gz // (nz // 2)
        self.mid = nz // 2 - 1 + self.side
        self.far = self.side * (nz - 1)
        self.is_mid = self.gz == self.mid
        self.is_far = jnp.logical_and(self.gz == self.far, jnp.logical_not(self.is_mid))

    def member(self, offset):
        q = lax.rem(self.group + offset, self.groups)
        return q, q // self.ny, lax.rem(q, self.ny)


def block(start, size):
    return pl.ds(pl.multiple_of(start, size), size)


def remote(src, dst, send, recv, **device):
    return pltpu.make_async_remote_copy(
        src_ref=src, dst_ref=dst, send_sem=send, recv_sem=recv, device_id=device, device_id_type=MESH
    )


def column(row):
    n = row.shape[1]
    same = lax.broadcasted_iota(jnp.int32, (n, n), 0) == lax.broadcasted_iota(jnp.int32, (n, n), 1)
    return jnp.sum(jnp.where(same, row, 0.0), axis=1, keepdims=True)


def turn_in(slab, source, count):
    def body(i, carry):
        for u in range(8):
            channel = i * 8 + u
            for part in range(slab.shape[0]):
                slab.at[part][pl.ds(channel * PITCH, GROUP), :] = source(channel, part).astype(
                    jnp.float32
                )
        return carry

    lax.fori_loop(0, count // 8, body, 0)


def turn_out(slab, put, count):
    def body(i, carry):
        for u in range(8):
            channel = i * 8 + u
            for part in range(slab.shape[0]):
                rows = slab.at[part][pl.ds(channel * PITCH, GROUP), :]
                put(channel, part, rows.astype(jnp.bfloat16))
        return carry

    lax.fori_loop(0, count // 8, body, 0)


def get_rows(slab, row, count):
    return jnp.concatenate(
        [
            slab.at[part][pl.ds(row + u, count, stride=PITCH), :]
            for u in range(WIDE)
            for part in range(slab.shape[0])
        ],
        axis=1,
    )


def put_rows(slab, row, values):
    parts = slab.shape[0]
    for u in range(WIDE):
        for part in range(parts):
            lane = (u * parts + part) * LANES
            slab.at[part][pl.ds(row + u, values.shape[0], stride=PITCH), :] = values[
                :, lane : lane + LANES
            ]


def start(copies):
    for copy, _ in copies:
        copy.start()


def drain(copies):
    for copy, is_local in copies:
        if is_local:
            copy.wait()
        else:
            copy.wait_send()


def update_kernel(
    dims,
    pair_ref,
    mask_ref,
    gain_row_ref,
    mix_gain_ref,
    w0_ref,
    w1_ref,
    w2_ref,
    w3_ref,
    w4_ref,
    w5_ref,
    out_ref,
    raw_ref,
    left_ref,
    gate_ref,
    right,
    mix,
    ring,
    left,
    right_stage,
    left_stage,
    gate_stage,
    mix_stage,
    in_slab,
    out_slab,
    left_slab,
    weight,
    mix_weight,
    mix_gain_parts,
    mix_gain,
    raw_send,
    raw_recv,
    load_sem,
    small_send,
    small_recv,
    right_send,
    left_send,
    right_recv,
    left_recv,
    gate_sem,
    left_sem,
    mix_send,
    mix_recv,
    out_send,
    out_recv,
    credit,
):
    nx, ny, nz, near, away = dims
    at = Place(nx, ny, nz)
    c, rows, k = pair_ref.shape
    h_z, c_all = w0_ref.shape
    h = h_z * nz
    chunks = rows // GROUP
    half = chunks // 2
    own_rows = rows // 2
    steps = half
    per = near + away
    ahead = min(6, chunks)
    lag = min(LAG, steps)
    parts = k // LANES
    other = 1 - at.side

    def mid_of(side):
        return nz // 2 - 1 + side


    def chunk_of(t, side):
        return lax.rem(t + side * half, chunks)

    def raw_copy(t, side):
        chunk = chunk_of(t, side)
        where = block(chunk * GROUP, GROUP)
        return remote(
            pair_ref.at[:, where],
            raw_ref.at[block(at.gz * c, c), where],
            raw_send.at[t, side],
            raw_recv.at[chunk, at.gz],
            gz=mid_of(side),
        )

    def arrive(t):
        chunk = chunk_of(t, at.side)
        where = block(chunk * GROUP, GROUP)
        for o in range(1, nz):
            z = lax.rem(at.gz + o, nz)
            landed = raw_ref.at[block(z * c, c), where]
            remote(landed, landed, raw_send.at[t, 0], raw_recv.at[chunk, z], gz=z).wait_recv()

    def loads(t):
        slot = lax.rem(t, 2)
        where = block(chunk_of(t, at.side) * GROUP, GROUP)
        found = []
        for o in range(nz):
            z = lax.rem(at.gz + o, nz)
            src = pair_ref.at[:, where] if o == 0 else raw_ref.at[block(z * c, c), where]
            found.append(
                pltpu.make_async_copy(src, ring.at[slot, block(z * c, c)], load_sem.at[slot, o])
            )
        return found

    def small(z):
        sources = (w0_ref, w1_ref, w2_ref, w3_ref, w4_ref)
        found = [(src, weight.at[index, block(z * h_z, h_z)]) for index, src in enumerate(sources)]
        found.append((w5_ref, mix_weight.at[block(z * c, c)]))
        found.append((mix_gain_ref, mix_gain_parts.at[z]))
        return list(enumerate(found))

    def small_copies(side):
        return [
            (
                remote(
                    src, dst, small_send.at[side, i], small_recv.at[at.gz, i], gz=mid_of(side)
                ),
                False,
            )
            for i, (src, dst) in small(at.gz)
        ]

    def small_own():
        return [
            (pltpu.make_async_copy(src, dst, small_recv.at[at.gz, i]), True)
            for i, (src, dst) in small(at.gz)
        ]

    def small_arrive():
        drain(small_own())
        for o in range(1, nz):
            z = lax.rem(at.gz + o, nz)
            for i, (src, dst) in small(z):
                remote(src, dst, small_send.at[0, i], small_recv.at[z, i], gz=z).wait_recv()
        for z in range(nz):
            mix_gain[z * h_z : (z + 1) * h_z, :] = column(mix_gain_parts[z])


    def sends(stage, out, first, send, recv, slot):
        where = (block(first, GROUP), block(at.gx * k, k))
        found = []
        for o in range(at.groups):
            q, qx, qy = at.member(o)
            if o > 0:
                found.append(
                    (
                        remote(
                            stage.at[slot, pl.ds(q * per, near)],
                            out.at[(pl.ds(0, near),) + where],
                            send.at[slot, o],
                            recv.at[at.group],
                            gx=qx,
                            gy=qy,
                        ),
                        False,
                    )
                )
            if away:
                found.append(
                    (
                        remote(
                            stage.at[slot, pl.ds(q * per + near, away)],
                            out.at[(pl.ds(0, away),) + where],
                            send.at[slot, at.groups + o],
                            recv.at[at.group],
                            gx=qx,
                            gy=qy,
                            gz=at.far,
                        ),
                        False,
                    )
                )
        return found

    def right_first(t):
        return at.gy * rows + chunk_of(t, at.side) * GROUP

    def left_first(t):
        return at.gy * own_rows + t * GROUP

    def right_sends(t):
        slot = lax.rem(t, SLOTS)
        return sends(right_stage, right, right_first(t), right_send, right_recv, slot)

    def left_sends(t):
        slot = lax.rem(t, SLOTS)
        own = pltpu.make_async_copy(
            left_stage.at[slot, pl.ds(at.group * per, near)],
            left_ref.at[pl.ds(0, near), block(left_first(t), GROUP), block(at.gx * k, k)],
            left_send.at[slot, 0],
        )
        return sends(left_stage, left_ref, left_first(t), left_send, left_recv, slot) + [(own, True)]

    def gate_out(t):
        slot = lax.rem(t, 2)
        return pltpu.make_async_copy(
            gate_stage.at[slot], gate_ref.at[pl.ds(t * GROUP, GROUP)], gate_sem.at[slot]
        )

    def project(t, with_left):
        slot = lax.rem(t, SLOTS)
        gate_slot = lax.rem(t, 2)
        load_slot = lax.rem(t, 2)
        r0 = chunk_of(t, at.side) * GROUP
        gain = column(gain_row_ref[...])
        turn_in(
            in_slab,
            lambda channel, part: ring[load_slot, channel, :, part * LANES : (part + 1) * LANES],
            c_all,
        )

        def body(i, carry):
            r = i * WIDE
            normed = normalize(get_rows(in_slab, r, c_all), gain)
            mask = jnp.concatenate(
                [mask_ref[pl.ds(r0 + r + u, 1), :] for u in range(WIDE)], axis=1
            ).astype(jnp.float32)

            def part(index):
                return jnp.dot(weight[index], normed, preferred_element_type=jnp.float32)

            put_rows(out_slab, r, mask * jax.nn.sigmoid(part(3)) * part(2))
            if with_left:
                put_rows(left_slab, r, mask * jax.nn.sigmoid(part(1)) * part(0))
                gates = jax.nn.sigmoid(part(4)).astype(jnp.bfloat16)
                for u in range(WIDE):
                    gate_stage[gate_slot, r + u] = gates[:, u * k : (u + 1) * k]
            return carry

        lax.fori_loop(0, GROUP // WIDE, body, 0)

        def stage_into(stage):
            def put(head, part, values):
                stage[slot, head, :, part * LANES : (part + 1) * LANES] = values

            return put

        turn_out(out_slab, stage_into(right_stage), h)
        right[0:near, block(right_first(t), GROUP), block(at.gx * k, k)] = right_stage[
            slot, pl.ds(at.group * per, near)
        ]
        if with_left:
            turn_out(left_slab, stage_into(left_stage), h)

    def collect(heads, first_offset):
        for o in range(first_offset, at.groups):
            q, qx, qy = at.member(o)
            for out, size, recv in ((right, rows, right_recv), (left_ref, own_rows, left_recv)):
                whole = out.at[pl.ds(0, heads), block(qy * size, size), block(qx * k, k)]
                remote(whole, whole, gate_sem.at[0], recv.at[q], gz=at.mid).wait_recv()


    def left_loads(t, heads):
        slot = lax.rem(t, 2)
        return [
            pltpu.make_async_copy(
                left_ref.at[pl.ds(0, heads), block(y * own_rows + t * GROUP, GROUP)],
                left.at[slot, pl.ds(0, heads), pl.ds(y * GROUP, GROUP)],
                left_sem.at[slot, y],
            )
            for y in range(ny)
        ]

    def mix_sends(t, heads, shift, first_offset):
        slot = lax.rem(t, SLOTS)
        found = []
        for o in range(first_offset, at.groups):
            q, qx, qy = at.member(o)
            found.append(
                (
                    remote(
                        mix_stage.at[
                            slot, pl.ds(0, heads), block(qy * GROUP, GROUP), block(qx * k, k)
                        ],
                        mix.at[pl.ds(at.group * per + shift, heads), block(t * GROUP, GROUP)],
                        mix_send.at[slot, o],
                        mix_recv.at[t],
                        gx=qx,
                        gy=qy,
                        gz=at.mid,
                    ),
                    False,
                )
            )
        return found

    def multiply(t, heads, shift, first_offset, paced=False):
        slot = lax.rem(t, SLOTS)
        left_slot = lax.rem(t, 2)

        @pl.when(t + 1 < steps)
        def _():
            for copy in left_loads(t + 1, heads):
                copy.start()

        for copy in left_loads(t, heads):
            copy.wait()

        @pl.when(t >= SLOTS)
        def _():
            drain(mix_sends(t - SLOTS, heads, shift, first_offset))

        def body(head, carry):
            product = lax.dot_general(
                left[left_slot, head],
                right[head],
                (((1,), (1,)), ((), ())),
                preferred_element_type=jnp.float32,
            )
            mix_stage[slot, head] = product.astype(jnp.bfloat16)
            return carry

        lax.fori_loop(0, heads, body, 0)
        if paced:

            @pl.when(t >= 1)
            def _():
                pl.semaphore_wait(credit, 1)

        start(mix_sends(t, heads, shift, first_offset))

    def multiply_end(heads, shift, first_offset):
        for t in range(max(steps - SLOTS, 0), steps):
            drain(mix_sends(t, heads, shift, first_offset))


    def gate_load(t):
        slot = lax.rem(t, 2)
        return pltpu.make_async_copy(
            gate_ref.at[pl.ds(t * GROUP, GROUP)], gate_stage.at[slot], gate_sem.at[slot]
        )

    def out_copies(t):
        slot = lax.rem(t, SLOTS)
        where = block(at.side * own_rows + t * GROUP, GROUP)
        own = pltpu.make_async_copy(
            right_stage.at[slot, block(at.gz * c, c)], out_ref.at[:, where], out_send.at[slot, 0]
        )
        found = [(own, True)]
        for o in range(1, nz):
            z = lax.rem(at.gz + o, nz)
            found.append(
                (
                    remote(
                        right_stage.at[slot, block(z * c, c)],
                        out_ref.at[:, where],
                        out_send.at[slot, o],
                        out_recv.at[at.side],
                        gz=z,
                    ),
                    False,
                )
            )
        return found

    def finish(t):
        slot = lax.rem(t, SLOTS)
        gate_slot = lax.rem(t, 2)
        here = block(t * GROUP, GROUP)
        if h > near:
            rest = mix.at[pl.ds(0, h - near), here]
            remote(rest, rest, out_send.at[0, 0], mix_recv.at[t], gz=at.mid).wait_recv()

        gain = mix_gain[...]
        turn_in(
            in_slab, lambda head, part: mix[head, here, part * LANES : (part + 1) * LANES], h
        )

        @pl.when(t + 1 < steps)
        def _():
            gate_load(t + 1).start()

        gate_load(t).wait()

        def body(i, carry):
            r = i * WIDE
            normed = normalize(get_rows(in_slab, r, h), gain)
            projected = jnp.dot(mix_weight[...], normed, preferred_element_type=jnp.float32)
            gates = jnp.concatenate([gate_stage[gate_slot, r + u] for u in range(WIDE)], axis=1)
            put_rows(out_slab, r, gates.astype(jnp.float32) * projected)
            return carry

        lax.fori_loop(0, GROUP // WIDE, body, 0)

        @pl.when(t >= SLOTS)
        def _():
            drain(out_copies(t - SLOTS))

        def put(channel, part, values):
            right_stage[slot, channel, :, part * LANES : (part + 1) * LANES] = values

        turn_out(out_slab, put, c_all)
        start(out_copies(t))


    @pl.when(jnp.logical_not(at.is_mid))
    def _():
        def begin(t, carry):
            raw_copy(t, 0).start()
            raw_copy(t, 1).start()
            return carry

        def end(t, carry):
            raw_copy(t, 0).wait_send()
            raw_copy(t, 1).wait_send()
            return carry

        for side in range(2):
            start(small_copies(side))
        lax.fori_loop(0, chunks, begin, 0)
        lax.fori_loop(0, chunks, end, 0)
        for side in range(2):
            drain(small_copies(side))

    if away:

        @pl.when(at.is_far)
        def _():
            collect(away, 0)
            for copy in left_loads(0, away):
                copy.start()

            def step(t, carry):
                multiply(t, away, near, 0, True)
                return carry

            lax.fori_loop(0, steps, step, 0)
            multiply_end(away, near, 0)

    @pl.when(at.is_mid)
    def _():
        start(small_own())
        start(small_copies(other))
        for t in range(ahead):
            raw_copy(t, other).start()
        small_arrive()
        arrive(0)
        for copy in loads(0):
            copy.start()

        def step(t, with_left):
            @pl.when(t + ahead < chunks)
            def _():
                raw_copy(t + ahead, other).start()

            @pl.when(t >= SLOTS)
            def _():
                drain(right_sends(t - SLOTS))
                if with_left:
                    drain(left_sends(t - SLOTS))

            if with_left:

                @pl.when(t >= 2)
                def _():
                    gate_out(t - 2).wait()

            for copy in loads(t):
                copy.wait()
            project(t, with_left)
            start(right_sends(t))
            if with_left:
                start(left_sends(t))
                gate_out(t).start()

            @pl.when(t + 1 < chunks)
            def _():
                arrive(t + 1)
                for copy in loads(t + 1):
                    copy.start()

        def first(t, carry):
            step(t, True)
            return carry

        def second(t, carry):
            step(t, False)
            return carry

        lax.fori_loop(0, half, first, 0)
        for t in range(max(half - 2, 0), half):
            gate_out(jnp.int32(t)).wait()
        gate_load(jnp.int32(0)).start()
        lax.fori_loop(half, chunks, second, 0)
        for t in range(max(half - SLOTS, 0), half):
            drain(left_sends(t))
        for t in range(max(chunks - SLOTS, 0), chunks):
            drain(right_sends(t))
        collect(near, 1)
        for copy in left_loads(0, near):
            copy.start()

        def both(t, carry):
            multiply(t, near, 0, 1)
            if away:

                @pl.when(t + 1 < steps)
                def _():
                    pl.semaphore_signal(
                        credit, inc=1, device_id={"gz": at.far}, device_id_type=MESH
                    )

            slot = lax.rem(t, SLOTS)
            mix[pl.ds(at.group * per, near), block(t * GROUP, GROUP)] = mix_stage[
                slot, 0:near, block(at.gy * GROUP, GROUP), block(at.gx * k, k)
            ]

            @pl.when(t >= lag)
            def _():
                finish(t - lag)

            return carry

        def last(t, carry):
            finish(t)
            return carry

        lax.fori_loop(0, steps, both, 0)
        lax.fori_loop(steps - lag, steps, last, 0)
        multiply_end(near, 0, 1)
        for t in range(max(steps - SLOTS, 0), steps):
            drain(out_copies(t))
        drain(small_copies(other))

        def end(t, carry):
            raw_copy(t, other).wait_send()
            return carry

        lax.fori_loop(0, chunks, end, 0)

    for side in range(2):

        @pl.when(at.gz != mid_of(side))
        def _():
            where = out_ref.at[:, pl.ds(side * own_rows, own_rows)]
            remote(where, where, gate_sem.at[0], out_recv.at[side], gz=mid_of(side)).wait_recv()


def local(
    pair,
    pair_mask,
    in_gain,
    w_left,
    w_left_gate,
    w_right,
    w_right_gate,
    w_out_gate,
    out_gain,
    w_out,
):
    nx, ny, nz = (lax.axis_size(a) for a in ("gx", "gy", "gz"))
    c, rows, k = pair.shape
    c_all = c * nz
    h = w_left.shape[1] * nz
    groups = nx * ny
    per = h // groups
    away = 0 if nz < 4 else max(1, per * 5 // 16)
    near = per - away
    deep = max(near, away)
    dims = (nx, ny, nz, near, away)
    chunks = rows // GROUP
    steps = chunks // 2
    parts = k // LANES
    widest = max(h, c_all)

    anywhere = pl.BlockSpec(memory_space=pl.ANY)
    whole = pl.BlockSpec(memory_space=pltpu.VMEM)
    shape = lambda *dims: jax.ShapeDtypeStruct(dims, jnp.bfloat16)
    half = lambda *dims: pltpu.VMEM(dims, jnp.bfloat16)
    full = lambda *dims: pltpu.VMEM(dims, jnp.float32)
    sem = pltpu.SemaphoreType.DMA

    return pl.pallas_call(
        functools.partial(update_kernel, dims),
        out_shape=(
            shape(c, rows, k),
            shape(c_all, rows, k),
            shape(deep, ny * rows // 2, nx * k),
            shape(rows // 2, h, k),
        ),
        in_specs=[anywhere, whole, whole] + [anywhere] * 7,
        out_specs=(anywhere,) * 4,
        scratch_shapes=[
            half(deep, ny * rows, nx * k),
            half(h, rows // 2, k),
            half(2, c_all, GROUP, k),
            half(2, deep, ny * GROUP, nx * k),
            half(SLOTS, widest, GROUP, k),
            half(SLOTS, h, GROUP, k),
            half(2, GROUP, h, k),
            half(SLOTS, deep, ny * GROUP, ny * rows),
            full(parts, widest * PITCH, LANES),
            full(parts, widest * PITCH, LANES),
            full(parts, h * PITCH, LANES),
            half(5, h, c_all),
            half(c_all, h),
            full(nz, 1, h // nz),
            full(h, 1),
            sem((chunks, 2)),
            sem((chunks, nz)),
            sem((2, nz)),
            sem((2, 7)),
            sem((nz, 7)),
            sem((SLOTS, 2 * groups)),
            sem((SLOTS, 2 * groups)),
            sem((groups,)),
            sem((groups,)),
            sem((2,)),
            sem((2, ny)),
            sem((SLOTS, groups)),
            sem((steps,)),
            sem((SLOTS, nz)),
            sem((2,)),
            pltpu.SemaphoreType.REGULAR,
        ],
        compiler_params=pltpu.CompilerParams(has_side_effects=True, vmem_limit_bytes=VMEM_LIMIT),
    )(
        pair,
        pair_mask,
        in_gain[None, :],
        out_gain[None, :],
        w_left.T,
        w_left_gate.T,
        w_right.T,
        w_right_gate.T,
        w_out_gate.T,
        w_out.T,
    )[0]


def solution(mesh):
    placed = (
        P("gz", "gy", "gx"),
        P("gy", "gx"),
        P(),
        P(None, "gz"),
        P(None, "gz"),
        P(None, "gz"),
        P(None, "gz"),
        P(None, "gz"),
        P("gz"),
        P(None, "gz"),
    )
    return jax.shard_map(
        local, mesh=mesh, in_specs=placed, out_specs=P("gz", "gy", "gx"), check_vma=False
    )
```

time: 1110 us -> 634 us (0.57)
  Pallas kernels: 994 us -> 623 us
  local copies, waits for them, and re-layouts: 70.6 us -> 7.65 us
  matrix products: 15.8 us -> 0 us
  blocking collectives: 15.8 us -> 0 us
  between operations: 14 us -> 0.01 us
    pallas_call x7 -> x1, Pallas kernels: 994 us -> 623 us  [local(): pl.pallas_call(functools.partial(update_kernel, dims), out_shape=(shape(c...]
    pallas_call x3 -> x0, local copies, waits for them, and re-layouts: 38.5 us -> none  [the longest x2 26.9 us: local(): pl.pallas_call(project_kernel, grid=(rows // block,), out_shape=(h_shape,...]
    dot_general x1 -> x0, matrix products: 15.8 us -> none  [local(): lax.dot_general(left_group, right_all, (((2,), (2,)), ((0,), (0,))), pref...]
    transpose x1 -> x0, local copies, waits for them, and re-layouts: 11.5 us -> none  [local(): return jnp.swapaxes(result, 0, 1)]
  transfers between devices with their start and end apart: 1 -> 0, of which waited for: 0 -> 0; matrix products, arithmetic and copies ran while one was open for 2% -> 0% of each run, Pallas kernels for 17% -> 0%
where the time goes in v3:
time: 634 us; the launch traced here: 631 us
  Pallas kernels  623 us (98%)
  local copies, waits for them, and re-layouts  7.65 us (1%)
    pallas_call x1, Pallas kernels, local(): pl.pallas_call(functools.partial(update_kernel, dims), out_shape=(shape(c...  623 us

profile of v3, /device:TPU:11, one launch (start us, length us, event | category | flops | bytes accessed | tf_op | source)
XLA Modules:
  0.0 630.6 jit_solution(229385581097261351)
XLA Ops:
  0.0 623.0 %shard_map.100 = (bf16[32,512,256]{2,1,0:T(8,128)(2,1)}, bf16[128,512,256]{2,1,0:T(8,128)(2,1)}, bf16[11,512,1024]{2,1,0:T(8,128)(2,1)}, bf16[256,128,256]{2,1,0:T(8,128)(2,1)}) custom-call(bf16[32,512,256]{2,1,0:T(8,128)(2,1)} %pair_ref.1, s32[512,256]{1,0:T(8,128)} %mask_ref.1, f32[1,128]{1,0:T(1,128)} %bitcast.14, f32[1,32]{1,0:T(1,128)} %bitcast.15, ...), custom_call_target="tpu_custom_call" | custom-call | tf_op jit(solution)/shard_map/pallas_call | solution.py:689
  623.0 7.7 %copy.12 = bf16[32,512,256]{2,1,0:T(8,128)(2,1)} copy(bf16[32,512,256]{2,1,0:T(8,128)(2,1)} %get-tuple-element.6) | data formatting | bytes 16777216

commit v4 on v3

--- a/solution.py
+++ b/solution.py
@@ -429,9 +429,7 @@
         lax.fori_loop(0, heads, body, 0)
         if paced:
 
-            @pl.when(t >= 1)
-            def _():
-                pl.semaphore_wait(credit, 1)
+            pl.semaphore_wait(credit, 1)
 
         start(mix_sends(t, heads, shift, first_offset))
 
@@ -610,11 +608,7 @@
             multiply(t, near, 0, 1)
             if away:
 
-                @pl.when(t + 1 < steps)
-                def _():
-                    pl.semaphore_signal(
-                        credit, inc=1, device_id={"gz": at.far}, device_id_type=MESH
-                    )
+                pl.semaphore_signal(credit, inc=1, device_id={"gz": at.far}, device_id_type=MESH)
 
             slot = lax.rem(t, SLOTS)
             mix[pl.ds(at.group * per, near), block(t * GROUP, GROUP)] = mix_stage[

time: 634 us -> 630 us (level)
  no operation moved by 1% of the time
where the time goes in v4:
time: 630 us; the launch traced here: 628 us
  Pallas kernels  620 us (98%)
  local copies, waits for them, and re-layouts  7.65 us (1%)
    pallas_call x1, Pallas kernels, local(): pl.pallas_call(functools.partial(update_kernel, dims), out_shape=(shape(c...  620 us

profile of v4, /device:TPU:11, one launch (start us, length us, event | category | flops | bytes accessed | tf_op | source)
XLA Modules:
  0.0 628.1 jit_solution(6918449712365082066)
XLA Ops:
  0.0 620.4 %shard_map.100 = (bf16[32,512,256]{2,1,0:T(8,128)(2,1)}, bf16[128,512,256]{2,1,0:T(8,128)(2,1)}, bf16[11,512,1024]{2,1,0:T(8,128)(2,1)}, bf16[256,128,256]{2,1,0:T(8,128)(2,1)}) custom-call(bf16[32,512,256]{2,1,0:T(8,128)(2,1)} %pair_ref.1, s32[512,256]{1,0:T(8,128)} %mask_ref.1, f32[1,128]{1,0:T(1,128)} %bitcast.14, f32[1,32]{1,0:T(1,128)} %bitcast.15, ...), custom_call_target="tpu_custom_call" | custom-call | tf_op jit(solution)/shard_map/pallas_call | solution.py:683
  620.5 7.7 %copy.12 = bf16[32,512,256]{2,1,0:T(8,128)(2,1)} copy(bf16[32,512,256]{2,1,0:T(8,128)(2,1)} %get-tuple-element.6) | data formatting | bytes 16777216

commit v5 on v4

--- a/solution.py
+++ b/solution.py
@@ -358,12 +358,19 @@
         if with_left:
             turn_out(left_slab, stage_into(left_stage), h)
 
-    def collect(heads, first_offset):
+    def collect(out, size, recv, heads, first_offset):
         for o in range(first_offset, at.groups):
             q, qx, qy = at.member(o)
-            for out, size, recv in ((right, rows, right_recv), (left_ref, own_rows, left_recv)):
-                whole = out.at[pl.ds(0, heads), block(qy * size, size), block(qx * k, k)]
-                remote(whole, whole, gate_sem.at[0], recv.at[q], gz=at.mid).wait_recv()
+            whole = out.at[pl.ds(0, heads), block(qy * size, size), block(qx * k, k)]
+            remote(whole, whole, gate_sem.at[0], recv.at[q], gz=at.mid).wait_recv()
+
+    def collect_left(heads, first_offset):
+        collect(left_ref, own_rows, left_recv, heads, first_offset)
+        for copy in left_loads(0, heads):
+            copy.start()
+
+    def collect_right(heads, first_offset):
+        collect(right, rows, right_recv, heads, first_offset)
 
 
     def left_loads(t, heads):
@@ -530,9 +537,8 @@
 
         @pl.when(at.is_far)
         def _():
-            collect(away, 0)
-            for copy in left_loads(0, away):
-                copy.start()
+            collect_left(away, 0)
+            collect_right(away, 0)
 
             def step(t, carry):
                 multiply(t, away, near, 0, True)
@@ -547,10 +553,10 @@
         start(small_copies(other))
         for t in range(ahead):
             raw_copy(t, other).start()
-        small_arrive()
         arrive(0)
         for copy in loads(0):
             copy.start()
+        small_arrive()
 
         def step(t, with_left):
             @pl.when(t + ahead < chunks)
@@ -598,11 +604,10 @@
         lax.fori_loop(half, chunks, second, 0)
         for t in range(max(half - SLOTS, 0), half):
             drain(left_sends(t))
+        collect_left(near, 1)
         for t in range(max(chunks - SLOTS, 0), chunks):
             drain(right_sends(t))
-        collect(near, 1)
-        for copy in left_loads(0, near):
-            copy.start()
+        collect_right(near, 1)
 
         def both(t, carry):
             multiply(t, near, 0, 1)

time: 630 us -> 629 us (level)
  no operation moved by 1% of the time
where the time goes in v5:
time: 629 us; the launch traced here: 627 us
  Pallas kernels  619 us (98%)
  local copies, waits for them, and re-layouts  7.65 us (1%)
    pallas_call x1, Pallas kernels, local(): pl.pallas_call(functools.partial(update_kernel, dims), out_shape=(shape(c...  619 us

profile of v5, /device:TPU:11, one launch (start us, length us, event | category | flops | bytes accessed | tf_op | source)
XLA Modules:
  0.0 627.0 jit_solution(11313374024312374531)
XLA Ops:
  0.0 619.3 %shard_map.100 = (bf16[32,512,256]{2,1,0:T(8,128)(2,1)}, bf16[128,512,256]{2,1,0:T(8,128)(2,1)}, bf16[11,512,1024]{2,1,0:T(8,128)(2,1)}, bf16[256,128,256]{2,1,0:T(8,128)(2,1)}) custom-call(bf16[32,512,256]{2,1,0:T(8,128)(2,1)} %pair_ref.1, s32[512,256]{1,0:T(8,128)} %mask_ref.1, f32[1,128]{1,0:T(1,128)} %bitcast.14, f32[1,32]{1,0:T(1,128)} %bitcast.15, ...), custom_call_target="tpu_custom_call" | custom-call | tf_op jit(solution)/shard_map/pallas_call | solution.py:688
  619.3 7.7 %copy.12 = bf16[32,512,256]{2,1,0:T(8,128)(2,1)} copy(bf16[32,512,256]{2,1,0:T(8,128)(2,1)} %get-tuple-element.6) | data formatting | bytes 16777216
